TPU v7x, 32 devices: a whole 2x2x4 slice. The times are simulated.
32 devices in a mesh: seq: 8 (over z, core), feat: 4 (over y, x).
Axes of the slice: x: 2, y: 2, z: 4, core: 2. Of those that a mesh axis runs over, the one named last changes fastest.
Arguments:
- activations: bfloat16 [2048, 6144], P('seq', 'feat'), may hold values from -15 to 15
- ridge_scale: float32 [], replicated, may hold values from 0.5 to 2
Outputs:
- whitened: bfloat16 [2048, 6144], P('seq', 'feat')
All inputs are finite; a program needn't handle non-finite values.
Results may differ from a plain program's by a relative error of at most 0.0033.
Values sent between devices are 32-bit elements; how exact they have to be, the bound alone decides.
A program may use at most 128 MiB of HBM per device.

v0:
```python
import jax
import jax.numpy as jnp
from jax import lax
from jax.sharding import PartitionSpec as P

RANK = 128
ROOT_STEPS = 12
precise = lax.Precision.HIGHEST


def partner_2(block, axis, bit):
    count = lax.axis_size(axis)
    route = []
    for low in range(count):
        high = low | 1 << bit
        if high != low and high < count:
            route += [(low, high), (high, low)]
    return lax.ppermute(block, axis, route)


def product(left_matrix, right_matrix):
    return jnp.dot(left_matrix, right_matrix, precision=precise)


def reduce_gram(stacked_gram):
    rank_size = stacked_gram.shape[0] // 2
    identity = jnp.eye(rank_size, dtype=stacked_gram.dtype)
    subspace = jnp.concatenate([identity, identity], axis=0) * 0.7071067811865476
    image_cols = product(stacked_gram, subspace)
    factor = jnp.linalg.cholesky(product(image_cols.T, image_cols))
    subspace = jax.scipy.linalg.solve_triangular(factor, image_cols.T, lower=True).T
    quotient = product(subspace.T, product(stacked_gram, subspace))
    quotient = 0.5 * (quotient + quotient.T)
    tail_mass = (jnp.trace(stacked_gram) - jnp.trace(quotient)) / rank_size
    root_factor = jnp.linalg.cholesky(quotient)
    inner_gram = product(root_factor.T, root_factor) + tail_mass * identity
    lower_factor = jnp.linalg.cholesky(inner_gram)
    return jax.scipy.linalg.solve_triangular(
        lower_factor, product(root_factor.T, subspace.T), lower=True
    )


def combine(earlier, later):
    own_gram, cross_gram, last_gram = lax.psum(
        (product(earlier, earlier.T), product(earlier, later.T), product(later, later.T)), "feat"
    )
    stacked_gram = jnp.concatenate(
        [jnp.concatenate([own_gram, cross_gram], 1), jnp.concatenate([cross_gram.T, last_gram], 1)],
        0,
    )
    mixing = reduce_gram(stacked_gram)
    return product(mixing, jnp.concatenate([earlier, later], 0))


def square_root(matrix):
    identity = jnp.eye(matrix.shape[0], dtype=matrix.dtype)
    norm_size = jnp.sqrt(jnp.sum(matrix * matrix))
    current = matrix / norm_size
    partner = identity
    for repeat in range(ROOT_STEPS):
        middle = 1.5 * identity - 0.5 * product(partner, current)
        current = product(current, middle)
        partner = product(middle, partner)
    return current * jnp.sqrt(norm_size)


def on_device(activations, ridge_scale):
    width = activations.shape[1]
    block_count = activations.shape[0] // (2 * RANK)
    block_rows = activations.reshape(block_count, 2 * RANK, width)
    partial_grams = jnp.einsum(
        "bik,bjk->bij", block_rows, block_rows, preferred_element_type=jnp.float32
    )
    slab_grams = lax.psum(partial_grams, "feat")
    mixtures = jax.vmap(reduce_gram)(slab_grams)
    sketches = jnp.einsum(
        "bij,bjk->bik", mixtures, block_rows.astype(jnp.float32), precision=precise
    )
    slab_sketch = sketches[0]
    levels = lax.axis_size("seq").bit_length() - 1
    seq_index = lax.axis_index("seq")
    tree_block = slab_sketch
    prefix = slab_sketch
    for tree_level in range(levels):
        partner = partner_2(tree_block, "seq", tree_level)
        merged = combine(partner, prefix)
        has_bit = seq_index // (1 << tree_level) % 2 == 1
        prefix = jnp.where(has_bit, merged, prefix)
        if tree_level + 1 < levels:
            tree_block = combine(tree_block, partner)
    seen_rows = ((seq_index + 1) * activations.shape[0]).astype(jnp.float32)
    scaled = prefix * lax.rsqrt(seen_rows * ridge_scale)
    half_basis = scaled.astype(jnp.bfloat16)
    small_gram, projection = lax.psum(
        (
            product(scaled, scaled.T),
            jnp.dot(activations, half_basis.T, preferred_element_type=jnp.float32),
        ),
        "feat",
    )
    identity = jnp.eye(small_gram.shape[0], dtype=small_gram.dtype)
    shifted = identity + small_gram
    total_gram = shifted + square_root(shifted)
    total_gram = 0.5 * (total_gram + total_gram.T)
    coefficients = jax.scipy.linalg.cho_solve(
        (jnp.linalg.cholesky(total_gram), True), projection.T
    ).T
    restored = jnp.dot(
        coefficients.astype(jnp.bfloat16), half_basis, preferred_element_type=jnp.float32
    )
    return ((activations.astype(jnp.float32) - restored) * lax.rsqrt(ridge_scale)).astype(
        jnp.bfloat16
    )


def solution(mesh):
    placed = (P("seq", "feat"), P())
    return jax.shard_map(
        on_device, mesh=mesh, in_specs=placed, out_specs=P("seq", "feat"), check_vma=False
    )
```

profile of v0, /device:TPU:0, one launch (start us, length us, event | category | flops | bytes accessed | tf_op | source)
XLA Modules:
  0.0 740.0 jit_solution(10634055439625661038)
XLA Ops:
  9.2 46.9 %all-reduce.10.cloned.1.call-done = f32[1,256,256]{2,1,0:T(8,128)} async-done(((f32[1,256,256]{2,1,0:T(8,128)}), f32[1,256,256]{2,1,0:T(8,128)}) %all-reduce.10.cloned.1.call-update) | async-done | bytes 262160 | tf_op jit(solution)/shard_map/psum | solution.py:74
  58.0 11.7 %custom-call.29 = f32[1,128,128]{2,1,0:T(8,128)S(1)} custom-call(f32[1,128,128]{2,1,0:T(8,128)S(1)} %fusion.75), custom_call_target="Cholesky" | custom-call | tf_op jit(solution)/shard_map/vmap(jit(cholesky))/cholesky | solution.py:30
  82.7 11.7 %custom-call.31 = f32[1,128,128]{2,1,0:T(8,128)S(1)} custom-call(f32[1,128,128]{2,1,0:T(8,128)S(1)} %fusion.121), custom_call_target="Cholesky" | custom-call | tf_op jit(solution)/shard_map/vmap(jit(cholesky))/cholesky | solution.py:35
  99.3 11.7 %custom-call.32 = f32[1,128,128]{2,1,0:T(8,128)S(1)} custom-call(f32[1,128,128]{2,1,0:T(8,128)S(1)} %fusion.73), custom_call_target="Cholesky" | custom-call | tf_op jit(solution)/shard_map/vmap(jit(cholesky))/cholesky | solution.py:37
  129.9 43.2 %all-reduce.18.cloned.1.call-done = (f32[128,128]{1,0:T(8,128)}, f32[128,128]{1,0:T(8,128)}, f32[128,128]{1,0:T(8,128)}, f32[128,128]{0,1:T(8,128)}) async-done(((f32[128,128]{1,0:T(8,128)}, f32[128,128]{1,0:T(8,128)}, f32[128,128]{1,0:T(8,128)}, f32[128,128]{0,1:T(8,128)}), (f32[128,128]{1,0:T(8,128)}, f32[128,128]{1,0:T(8,128)}, f32[128,128]{1,0:T(8,128)}, ...) | async-done | bytes 262160 | tf_op jit(solution)/shard_map/psum | solution.py:44
  178.1 11.7 %cholesky.404 = f32[128,128]{1,0:T(8,128)S(1)} custom-call(f32[128,128]{1,0:T(8,128)S(1)} %fusion.101), custom_call_target="Cholesky" | custom-call | tf_op jit(solution)/shard_map/jit(cholesky)/cholesky | solution.py:30
  202.7 12.1 %cholesky.415 = f32[128,128]{1,0:T(8,128)S(1)} custom-call(f32[128,128]{1,0:T(8,128)S(1)} %fusion.98), custom_call_target="Cholesky" | custom-call | tf_op jit(solution)/shard_map/jit(cholesky)/cholesky | solution.py:35
  218.7 11.7 %cholesky.426 = f32[128,128]{1,0:T(8,128)S(1)} custom-call(f32[128,128]{1,0:T(8,128)S(1)} %fusion.97), custom_call_target="Cholesky" | custom-call | tf_op jit(solution)/shard_map/jit(cholesky)/cholesky | solution.py:37
  242.1 11.7 %cholesky.338 = f32[128,128]{1,0:T(8,128)S(1)} custom-call(f32[128,128]{1,0:T(8,128)S(1)} %fusion.115), custom_call_target="Cholesky" | custom-call | tf_op jit(solution)/shard_map/jit(cholesky)/cholesky | solution.py:30
  267.0 11.7 %cholesky.349 = f32[128,128]{1,0:T(8,128)S(1)} custom-call(f32[128,128]{1,0:T(8,128)S(1)} %fusion.112), custom_call_target="Cholesky" | custom-call | tf_op jit(solution)/shard_map/jit(cholesky)/cholesky | solution.py:35
  282.5 11.7 %cholesky.360 = f32[128,128]{1,0:T(8,128)S(1)} custom-call(f32[128,128]{1,0:T(8,128)S(1)} %fusion.111), custom_call_target="Cholesky" | custom-call | tf_op jit(solution)/shard_map/jit(cholesky)/cholesky | solution.py:37
  312.8 13.1 %collective-permute-done.1 = f32[128,1536]{1,0:T(8,128)S(1)} collective-permute-done((f32[128,1536]{1,0:T(8,128)S(1)}, f32[128,1536]{1,0:T(8,128)S(1)}, u32[]{:S(2)}, u32[]{:S(2)}) %collective-permute-start.1) | collective-permute-done | bytes 786464 | tf_op jit(solution)/shard_map/ppermute | solution.py:18
  330.4 44.5 %all-reduce.16.cloned.1.call-done = (f32[128,128]{1,0:T(8,128)}, f32[128,128]{0,1:T(8,128)}, f32[128,128]{0,1:T(8,128)}, f32[128,128]{0,1:T(8,128)}, f32[128,128]{0,1:T(8,128)}) async-done(((f32[128,128]{1,0:T(8,128)}, f32[128,128]{0,1:T(8,128)}, f32[128,128]{0,1:T(8,128)}, f32[128,128]{0,1:T(8,128)}, f32[128,128]{0,1:T(8,128)}), (f32[128,128]{1,0:T(8,128)}, f32[128,128]{0,1:T(8,128)}, ...) | async-done | bytes 327696 | tf_op jit(solution)/shard_map/psum | solution.py:44
  378.5 11.7 %cholesky.437 = f32[128,128]{1,0:T(8,128)S(1)} custom-call(f32[128,128]{1,0:T(8,128)S(1)} %fusion.94), custom_call_target="Cholesky" | custom-call | tf_op jit(solution)/shard_map/jit(cholesky)/cholesky | solution.py:30
  403.2 11.7 %cholesky.448 = f32[128,128]{1,0:T(8,128)S(1)} custom-call(f32[128,128]{1,0:T(8,128)S(1)} %fusion.91), custom_call_target="Cholesky" | custom-call | tf_op jit(solution)/shard_map/jit(cholesky)/cholesky | solution.py:35
  418.9 11.7 %cholesky.459 = f32[128,128]{1,0:T(8,128)S(1)} custom-call(f32[128,128]{1,0:T(8,128)S(1)} %fusion.90), custom_call_target="Cholesky" | custom-call | tf_op jit(solution)/shard_map/jit(cholesky)/cholesky | solution.py:37
  432.5 11.7 %cholesky.371 = f32[128,128]{1,0:T(8,128)S(1)} custom-call(f32[128,128]{1,0:T(8,128)S(1)} %fusion.108), custom_call_target="Cholesky" | custom-call | tf_op jit(solution)/shard_map/jit(cholesky)/cholesky | solution.py:30
  458.0 11.7 %cholesky.382 = f32[128,128]{1,0:T(8,128)S(1)} custom-call(f32[128,128]{1,0:T(8,128)S(1)} %fusion.105), custom_call_target="Cholesky" | custom-call | tf_op jit(solution)/shard_map/jit(cholesky)/cholesky | solution.py:35
  474.5 11.7 %cholesky.393 = f32[128,128]{1,0:T(8,128)S(1)} custom-call(f32[128,128]{1,0:T(8,128)S(1)} %fusion.104), custom_call_target="Cholesky" | custom-call | tf_op jit(solution)/shard_map/jit(cholesky)/cholesky | solution.py:37
  515.4 21.0 %collective-permute-done.2 = f32[128,1536]{1,0:T(8,128)S(1)} collective-permute-done((f32[128,1536]{1,0:T(8,128)}, f32[128,1536]{1,0:T(8,128)S(1)}, u32[]{:S(2)}, u32[]{:S(2)}) %collective-permute-start.2) | collective-permute-done | bytes 786464 | tf_op jit(solution)/shard_map/ppermute | solution.py:18
  540.0 42.5 %all-reduce.14.cloned.1.call-done = (f32[128,128]{1,0:T(8,128)}, f32[128,128]{0,1:T(8,128)}, f32[128,128]{0,1:T(8,128)}) async-done(((f32[128,128]{1,0:T(8,128)}, f32[128,128]{0,1:T(8,128)}, f32[128,128]{0,1:T(8,128)}), (f32[128,128]{1,0:T(8,128)}, f32[128,128]{0,1:T(8,128)}, f32[128,128]{0,1:T(8,128)})) %all-reduce.14.cloned.1.call-update) | async-done | bytes 196624 | tf_op jit(solution)/shard_map/psum | solution.py:44
  586.1 11.7 %cholesky.470 = f32[128,128]{1,0:T(8,128)S(1)} custom-call(f32[128,128]{1,0:T(8,128)S(1)} %fusion.87), custom_call_target="Cholesky" | custom-call | tf_op jit(solution)/shard_map/jit(cholesky)/cholesky | solution.py:30
  653.8 42.6 %all-reduce.12.cloned.1.call-done = (f32[128,256]{1,0:T(8,128)}, f32[128,128]{0,1:T(8,128)}) async-done(((f32[128,256]{1,0:T(8,128)}, f32[128,128]{0,1:T(8,128)}), (f32[128,256]{1,0:T(8,128)}, f32[128,128]{0,1:T(8,128)})) %all-reduce.12.cloned.1.call-update) | async-done | bytes 196624 | tf_op jit(solution)/shard_map/psum | solution.py:94
  708.5 11.7 %cholesky.503 = f32[128,128]{1,0:T(8,128)S(1)} custom-call(f32[128,128]{1,0:T(8,128)S(1)} %copy.70), custom_call_target="Cholesky" | custom-call | tf_op jit(solution)/shard_map/jit(cholesky)/cholesky | solution.py:106
  (300 shorter events, 262.8 us)
Async XLA Ops:
  6.5 49.5 %all-reduce.10.cloned.1.call-start = ((), (), s32[]{:S(2)}) async-start(), calls=%async_computation | async-start | bytes 524288 | tf_op jit(solution)/shard_map/psum | solution.py:74
  9.1 164.0 %all-reduce.18.cloned.1.call-start = ((), (), s32[]{:S(2)}) async-start(), calls=%async_computation.4 | async-start | bytes 524288 | tf_op jit(solution)/shard_map/psum | solution.py:44
  56.1 25.1 %copy-start.6 = (f32[1,256,256]{2,1,0:T(8,128)S(1)}, f32[1,256,256]{2,1,0:T(8,128)}, u32[]{:S(2)}) copy-start(f32[1,256,256]{2,1,0:T(8,128)} %all-reduce.10.cloned.1.call-done) | copy-start | bytes 786436
  95.1 27.4 %copy-start.2 = (bf16[256,1536]{1,0:T(8,128)(2,1)S(1)}, bf16[256,1536]{1,0:T(8,128)(2,1)}, u32[]{:S(2)}) copy-start(bf16[256,1536]{1,0:T(8,128)(2,1)} %param.8) | copy-start | bytes 2359300
  123.0 2.4 collective-permute-start
  129.6 245.3 %all-reduce.16.cloned.1.call-start = ((), (), s32[]{:S(2)}) async-start(), calls=%async_computation.3 | async-start | bytes 655360 | tf_op jit(solution)/shard_map/psum | solution.py:44
  173.1 2.9 copy-start.8
  173.1 2.9 copy-start.9
  173.1 2.9 copy-start.12
  173.1 3.3 copy-start.11
  307.1 21.6 %copy-start = (f32[128,1536]{1,0:T(8,128)}, f32[128,1536]{1,0:T(8,128)S(1)}, u32[]{:S(2)}) copy-start(f32[128,1536]{1,0:T(8,128)S(1)} %fusion.3) | copy-start | bytes 2359300
  307.1 18.8 %collective-permute-start.1 = (f32[128,1536]{1,0:T(8,128)S(1)}, f32[128,1536]{1,0:T(8,128)S(1)}, u32[]{:S(2)}, u32[]{:S(2)}) collective-permute-start(f32[128,1536]{1,0:T(8,128)S(1)} %fusion.3), channel_id=1, source_target_pairs={{0,8},{8,0},{4,12},{12,4},{16,24},{24,16},{20,28},{28,20},{1,9},{9... | collective-permute-start | bytes 2359304 | tf_op jit(solution)/shard_map/ppermute | solution.py:18
  330.2 252.4 %all-reduce.14.cloned.1.call-start = ((), (), s32[]{:S(2)}) async-start(), calls=%async_computation.2 | async-start | bytes 393216 | tf_op jit(solution)/shard_map/psum | solution.py:44
  374.9 2.3 copy-start.14
  374.9 2.3 copy-start.18
  402.3 29.0 %copy-start.7 = (f32[128,128]{0,1:T(8,128)S(1)}, f32[128,128]{0,1:T(8,128)}, u32[]{:S(2)}) copy-start(f32[128,128]{0,1:T(8,128)} %get-tuple-element.19) | copy-start | bytes 196612
  402.4 29.0 %copy-start.10 = (f32[128,128]{0,1:T(8,128)S(1)}, f32[128,128]{0,1:T(8,128)}, u32[]{:S(2)}) copy-start(f32[128,128]{0,1:T(8,128)} %get-tuple-element.18) | copy-start | bytes 196612
  402.4 29.0 %copy-start.16 = (f32[128,128]{0,1:T(8,128)S(1)}, f32[128,128]{0,1:T(8,128)}, u32[]{:S(2)}) copy-start(f32[128,128]{0,1:T(8,128)} %get-tuple-element.20) | copy-start | bytes 196612
  470.4 27.4 %copy-start.1 = (f32[128,1536]{1,0:T(8,128)S(1)}, f32[128,1536]{1,0:T(8,128)}, u32[]{:S(2)}) copy-start(f32[128,1536]{1,0:T(8,128)} %copy-done) | copy-start | bytes 2359300
  499.7 36.7 %collective-permute-start.2 = (f32[128,1536]{1,0:T(8,128)}, f32[128,1536]{1,0:T(8,128)S(1)}, u32[]{:S(2)}, u32[]{:S(2)}) collective-permute-start(f32[128,1536]{1,0:T(8,128)} %fusion.7), channel_id=1, source_target_pairs={{0,16},{16,0},{4,20},{20,4},{8,24},{24,8},{12,28},{28,12},{1,17},{... | collective-permute-start | bytes 2359304 | tf_op jit(solution)/shard_map/ppermute | solution.py:18
  539.3 157.2 %all-reduce.12.cloned.1.call-start = ((), (), s32[]{:S(2)}) async-start(), calls=%async_computation.1 | async-start | bytes 393216 | tf_op jit(solution)/shard_map/psum | solution.py:94
  582.5 2.3 copy-start.17
  610.6 39.4 %copy-start.5 = (f32[128,1536]{1,0:T(8,128)S(1)}, f32[128,1536]{1,0:T(8,128)}, u32[]{:S(2)}) copy-start(f32[128,1536]{1,0:T(8,128)} %copy-done.4) | copy-start | bytes 2359300
  707.2 24.2 %copy-start.19 = (f32[128,256]{1,0:T(8,128)S(1)}, f32[128,256]{1,0:T(8,128)}, u32[]{:S(2)}) copy-start(f32[128,256]{1,0:T(8,128)} %get-tuple-element.10) | copy-start | bytes 393220
  (4 other events, 6.8 us)
Sparse Core Ops, SparseCore 0:
  10.3 45.7 all-reduce.9
  129.7 43.3 all-reduce.17
  330.3 44.6 all-reduce.15
  539.4 43.1 all-reduce.13
  653.8 42.6 all-reduce.11
where the time goes:
time: 750 us; the launch traced here: 740 us
  other arithmetic  385 us (51%)
  waiting for transfers between devices  255 us (34%)
  matrix products  66.9 us (9%)
  between operations  23.9 us (3%)
    psum x3, waiting for transfers between devices, combine(): lax.psum((product(earlier, earlier.T), product(earlier, later.T), product...  130 us
    another operation x18, other arithmetic, reduce_gram(): root_factor = jnp.linalg.cholesky(quotient)  74.9 us
    another operation x18, other arithmetic, reduce_gram(): lower_factor = jnp.linalg.cholesky(inner_gram)  74.6 us
    another operation x18, other arithmetic, reduce_gram(): factor = jnp.linalg.cholesky(product(image_cols.T, image_cols))  74.4 us
    another operation x12, other arithmetic, reduce_gram(): jax.scipy.linalg.solve_triangular(lower_factor, product(root_factor.T, su...  63.4 us
    another operation x12, other arithmetic, reduce_gram(): jax.scipy.linalg.solve_triangular(factor, image_cols.T, lower=True)  62.9 us
    dot_general x89, matrix products, product(): return jnp.dot(left_matrix, right_matrix, precision=precise)  57.2 us
    psum x1, waiting for transfers between devices, on_device(): slab_grams = lax.psum(partial_grams, 'feat')  46.9 us
  transfers between devices with their start and end apart: 8, of which 8 were waited for; matrix products, arithmetic and copies ran while one was open for 3% of the time, Pallas kernels for 0%

commit v1 on v0

--- a/solution.py
+++ b/solution.py
@@ -71,7 +71,7 @@
     partial_grams = jnp.einsum(
         "bik,bjk->bij", block_rows, block_rows, preferred_element_type=jnp.float32
     )
-    slab_grams = lax.psum(partial_grams, "feat")
+    slab_grams = jnp.sum(lax.all_gather(partial_grams, "feat"), axis=0)
     mixtures = jax.vmap(reduce_gram)(slab_grams)
     sketches = jnp.einsum(
         "bij,bjk->bik", mixtures, block_rows.astype(jnp.float32), precision=precise

time: 750 us -> 735 us (0.980)
  waiting for transfers between devices: 255 us -> 237 us
    psum x1 -> x0, waiting for transfers between devices: 46.9 us -> none  [on_device(): slab_grams = lax.psum(partial_grams, 'feat')]
    all_gather x0 -> x1, waiting for transfers between devices: none -> 29.3 us  [on_device(): slab_grams = jnp.sum(lax.all_gather(partial_grams, 'feat'), axis=0)]
where the time goes in v1:
time: 735 us; the launch traced here: 725 us
  other arithmetic  388 us (53%)
  waiting for transfers between devices  237 us (32%)
  matrix products  66.8 us (9%)
  between operations  24 us (3%)
    psum x3, waiting for transfers between devices, combine(): lax.psum((product(earlier, earlier.T), product(earlier, later.T), product...  130 us
    another operation x18, other arithmetic, reduce_gram(): root_factor = jnp.linalg.cholesky(quotient)  74.9 us
    another operation x18, other arithmetic, reduce_gram(): lower_factor = jnp.linalg.cholesky(inner_gram)  74.6 us
    another operation x18, other arithmetic, reduce_gram(): factor = jnp.linalg.cholesky(product(image_cols.T, image_cols))  74.5 us
    another operation x12, other arithmetic, reduce_gram(): jax.scipy.linalg.solve_triangular(lower_factor, product(root_factor.T, su...  63.4 us
    another operation x12, other arithmetic, reduce_gram(): jax.scipy.linalg.solve_triangular(factor, image_cols.T, lower=True)  62.9 us
    dot_general x89, matrix products, product(): return jnp.dot(left_matrix, right_matrix, precision=precise)  57.1 us
    psum x1, waiting for transfers between devices, on_device(): lax.psum((product(scaled, scaled.T), jnp.dot(activations, half_basis.T, p...  42.6 us
  transfers between devices with their start and end apart: 8, of which 8 were waited for; matrix products, arithmetic and copies ran while one was open for 3% of the time, Pallas kernels for 0%

profile of v1, /device:TPU:0, one launch (start us, length us, event | category | flops | bytes accessed | tf_op | source)
XLA Modules:
  0.0 725.3 jit_solution(8483613415419710054)
XLA Ops:
  9.1 29.3 %all-gather.3.cloned.1.call-done = f32[1024,256]{1,0:T(8,128)} async-done(((f32[256,256]{1,0:T(8,128)}), f32[1024,256]{1,0:T(8,128)}) %all-gather.3.cloned.1.call-update) | async-done | bytes 1048592 | tf_op jit(solution)/shard_map/all_gather | solution.py:74
  41.3 11.7 %custom-call.29 = f32[1,128,128]{2,1,0:T(8,128)S(1)} custom-call(f32[1,128,128]{2,1,0:T(8,128)S(1)} %fusion.72), custom_call_target="Cholesky" | custom-call | tf_op jit(solution)/shard_map/vmap(jit(cholesky))/cholesky | solution.py:30
  66.0 11.7 %custom-call.31 = f32[1,128,128]{2,1,0:T(8,128)S(1)} custom-call(f32[1,128,128]{2,1,0:T(8,128)S(1)} %fusion.118), custom_call_target="Cholesky" | custom-call | tf_op jit(solution)/shard_map/vmap(jit(cholesky))/cholesky | solution.py:35
  81.9 11.7 %custom-call.32 = f32[1,128,128]{2,1,0:T(8,128)S(1)} custom-call(f32[1,128,128]{2,1,0:T(8,128)S(1)} %fusion.70), custom_call_target="Cholesky" | custom-call | tf_op jit(solution)/shard_map/vmap(jit(cholesky))/cholesky | solution.py:37
  112.5 43.2 %all-reduce.15.cloned.1.call-done = (f32[128,128]{1,0:T(8,128)}, f32[128,128]{1,0:T(8,128)}, f32[128,128]{1,0:T(8,128)}, f32[128,128]{0,1:T(8,128)}) async-done(((f32[128,128]{1,0:T(8,128)}, f32[128,128]{1,0:T(8,128)}, f32[128,128]{1,0:T(8,128)}, f32[128,128]{0,1:T(8,128)}), (f32[128,128]{1,0:T(8,128)}, f32[128,128]{1,0:T(8,128)}, f32[128,128]{1,0:T(8,128)}, ...) | async-done | bytes 262160 | tf_op jit(solution)/shard_map/psum | solution.py:44
  161.5 11.7 %cholesky.404 = f32[128,128]{1,0:T(8,128)S(1)} custom-call(f32[128,128]{1,0:T(8,128)S(1)} %fusion.98), custom_call_target="Cholesky" | custom-call | tf_op jit(solution)/shard_map/jit(cholesky)/cholesky | solution.py:30
  186.2 12.1 %cholesky.415 = f32[128,128]{1,0:T(8,128)S(1)} custom-call(f32[128,128]{1,0:T(8,128)S(1)} %fusion.95), custom_call_target="Cholesky" | custom-call | tf_op jit(solution)/shard_map/jit(cholesky)/cholesky | solution.py:35
  202.2 11.7 %cholesky.426 = f32[128,128]{1,0:T(8,128)S(1)} custom-call(f32[128,128]{1,0:T(8,128)S(1)} %fusion.94), custom_call_target="Cholesky" | custom-call | tf_op jit(solution)/shard_map/jit(cholesky)/cholesky | solution.py:37
  225.6 11.7 %cholesky.338 = f32[128,128]{1,0:T(8,128)S(1)} custom-call(f32[128,128]{1,0:T(8,128)S(1)} %fusion.112), custom_call_target="Cholesky" | custom-call | tf_op jit(solution)/shard_map/jit(cholesky)/cholesky | solution.py:30
  250.4 11.7 %cholesky.349 = f32[128,128]{1,0:T(8,128)S(1)} custom-call(f32[128,128]{1,0:T(8,128)S(1)} %fusion.109), custom_call_target="Cholesky" | custom-call | tf_op jit(solution)/shard_map/jit(cholesky)/cholesky | solution.py:35
  266.0 11.7 %cholesky.360 = f32[128,128]{1,0:T(8,128)S(1)} custom-call(f32[128,128]{1,0:T(8,128)S(1)} %fusion.108), custom_call_target="Cholesky" | custom-call | tf_op jit(solution)/shard_map/jit(cholesky)/cholesky | solution.py:37
  296.2 13.1 %collective-permute-done.1 = f32[128,1536]{1,0:T(8,128)S(1)} collective-permute-done((f32[128,1536]{1,0:T(8,128)S(1)}, f32[128,1536]{1,0:T(8,128)S(1)}, u32[]{:S(2)}, u32[]{:S(2)}) %collective-permute-start.1) | collective-permute-done | bytes 786464 | tf_op jit(solution)/shard_map/ppermute | solution.py:18
  313.9 44.5 %all-reduce.13.cloned.1.call-done = (f32[128,128]{1,0:T(8,128)}, f32[128,128]{0,1:T(8,128)}, f32[128,128]{0,1:T(8,128)}, f32[128,128]{0,1:T(8,128)}, f32[128,128]{0,1:T(8,128)}) async-done(((f32[128,128]{1,0:T(8,128)}, f32[128,128]{0,1:T(8,128)}, f32[128,128]{0,1:T(8,128)}, f32[128,128]{0,1:T(8,128)}, f32[128,128]{0,1:T(8,128)}), (f32[128,128]{1,0:T(8,128)}, f32[128,128]{0,1:T(8,128)}, ...) | async-done | bytes 327696 | tf_op jit(solution)/shard_map/psum | solution.py:44
  362.7 11.7 %cholesky.437 = f32[128,128]{1,0:T(8,128)S(1)} custom-call(f32[128,128]{1,0:T(8,128)S(1)} %fusion.91), custom_call_target="Cholesky" | custom-call | tf_op jit(solution)/shard_map/jit(cholesky)/cholesky | solution.py:30
  387.4 11.7 %cholesky.448 = f32[128,128]{1,0:T(8,128)S(1)} custom-call(f32[128,128]{1,0:T(8,128)S(1)} %fusion.88), custom_call_target="Cholesky" | custom-call | tf_op jit(solution)/shard_map/jit(cholesky)/cholesky | solution.py:35
  403.4 11.7 %cholesky.459 = f32[128,128]{1,0:T(8,128)S(1)} custom-call(f32[128,128]{1,0:T(8,128)S(1)} %fusion.87), custom_call_target="Cholesky" | custom-call | tf_op jit(solution)/shard_map/jit(cholesky)/cholesky | solution.py:37
  417.0 11.7 %cholesky.371 = f32[128,128]{1,0:T(8,128)S(1)} custom-call(f32[128,128]{1,0:T(8,128)S(1)} %fusion.105), custom_call_target="Cholesky" | custom-call | tf_op jit(solution)/shard_map/jit(cholesky)/cholesky | solution.py:30
  442.5 11.7 %cholesky.382 = f32[128,128]{1,0:T(8,128)S(1)} custom-call(f32[128,128]{1,0:T(8,128)S(1)} %fusion.102), custom_call_target="Cholesky" | custom-call | tf_op jit(solution)/shard_map/jit(cholesky)/cholesky | solution.py:35
  458.9 11.7 %cholesky.393 = f32[128,128]{1,0:T(8,128)S(1)} custom-call(f32[128,128]{1,0:T(8,128)S(1)} %fusion.101), custom_call_target="Cholesky" | custom-call | tf_op jit(solution)/shard_map/jit(cholesky)/cholesky | solution.py:37
  499.8 21.0 %collective-permute-done.2 = f32[128,1536]{1,0:T(8,128)S(1)} collective-permute-done((f32[128,1536]{1,0:T(8,128)}, f32[128,1536]{1,0:T(8,128)S(1)}, u32[]{:S(2)}, u32[]{:S(2)}) %collective-permute-start.2) | collective-permute-done | bytes 786464 | tf_op jit(solution)/shard_map/ppermute | solution.py:18
  524.4 42.5 %all-reduce.11.cloned.1.call-done = (f32[128,128]{1,0:T(8,128)}, f32[128,128]{0,1:T(8,128)}, f32[128,128]{0,1:T(8,128)}) async-done(((f32[128,128]{1,0:T(8,128)}, f32[128,128]{0,1:T(8,128)}, f32[128,128]{0,1:T(8,128)}), (f32[128,128]{1,0:T(8,128)}, f32[128,128]{0,1:T(8,128)}, f32[128,128]{0,1:T(8,128)})) %all-reduce.11.cloned.1.call-update) | async-done | bytes 196624 | tf_op jit(solution)/shard_map/psum | solution.py:44
  571.2 11.7 %cholesky.470 = f32[128,128]{1,0:T(8,128)S(1)} custom-call(f32[128,128]{1,0:T(8,128)S(1)} %fusion.84), custom_call_target="Cholesky" | custom-call | tf_op jit(solution)/shard_map/jit(cholesky)/cholesky | solution.py:30
  639.1 42.6 %all-reduce.9.cloned.1.call-done = (f32[128,256]{1,0:T(8,128)}, f32[128,128]{0,1:T(8,128)}) async-done(((f32[128,256]{1,0:T(8,128)}, f32[128,128]{0,1:T(8,128)}), (f32[128,256]{1,0:T(8,128)}, f32[128,128]{0,1:T(8,128)})) %all-reduce.9.cloned.1.call-update) | async-done | bytes 196624 | tf_op jit(solution)/shard_map/psum | solution.py:94
  693.8 11.7 %cholesky.503 = f32[128,128]{1,0:T(8,128)S(1)} custom-call(f32[128,128]{1,0:T(8,128)S(1)} %copy.70), custom_call_target="Cholesky" | custom-call | tf_op jit(solution)/shard_map/jit(cholesky)/cholesky | solution.py:106
  (299 shorter events, 265.6 us)
Async XLA Ops:
  6.5 31.9 %all-gather.3.cloned.1.call-start = ((), (), s32[]{:S(2)}) async-start(), calls=%async_computation | async-start | bytes 1310720 | tf_op jit(solution)/shard_map/all_gather | solution.py:74
  9.0 146.7 %all-reduce.15.cloned.1.call-start = ((), (), s32[]{:S(2)}) async-start(), calls=%async_computation.4 | async-start | bytes 524288 | tf_op jit(solution)/shard_map/psum | solution.py:44
  65.1 40.0 %copy-start.2 = (bf16[256,1536]{1,0:T(8,128)(2,1)S(1)}, bf16[256,1536]{1,0:T(8,128)(2,1)}, u32[]{:S(2)}) copy-start(bf16[256,1536]{1,0:T(8,128)(2,1)} %param.8) | copy-start | bytes 2359300
  105.6 2.4 collective-permute-start
  112.2 246.2 %all-reduce.13.cloned.1.call-start = ((), (), s32[]{:S(2)}) async-start(), calls=%async_computation.3 | async-start | bytes 655360 | tf_op jit(solution)/shard_map/psum | solution.py:44
  155.7 4.2 copy-start.7
  155.7 4.2 copy-start.8
  155.7 4.2 copy-start.10
  155.7 4.2 copy-start.11
  290.5 21.6 %copy-start = (f32[128,1536]{1,0:T(8,128)}, f32[128,1536]{1,0:T(8,128)S(1)}, u32[]{:S(2)}) copy-start(f32[128,1536]{1,0:T(8,128)S(1)} %fusion.3) | copy-start | bytes 2359300
  290.5 18.8 %collective-permute-start.1 = (f32[128,1536]{1,0:T(8,128)S(1)}, f32[128,1536]{1,0:T(8,128)S(1)}, u32[]{:S(2)}, u32[]{:S(2)}) collective-permute-start(f32[128,1536]{1,0:T(8,128)S(1)} %fusion.3), channel_id=1, source_target_pairs={{0,8},{8,0},{4,12},{12,4},{16,24},{24,16},{20,28},{28,20},{1,9},{9... | collective-permute-start | bytes 2359304 | tf_op jit(solution)/shard_map/ppermute | solution.py:18
  313.6 253.4 %all-reduce.11.cloned.1.call-start = ((), (), s32[]{:S(2)}) async-start(), calls=%async_computation.2 | async-start | bytes 393216 | tf_op jit(solution)/shard_map/psum | solution.py:44
  359.3 26.6 %copy-start.13 = (f32[128,128]{0,1:T(8,128)S(1)}, f32[128,128]{0,1:T(8,128)}, u32[]{:S(2)}) copy-start(f32[128,128]{0,1:T(8,128)} %get-tuple-element.17) | copy-start | bytes 196612
  359.3 26.6 %copy-start.17 = (f32[128,128]{1,0:T(8,128)S(1)}, f32[128,128]{1,0:T(8,128)}, u32[]{:S(2)}) copy-start(f32[128,128]{1,0:T(8,128)} %get-tuple-element.16) | copy-start | bytes 196612
  386.2 29.6 %copy-start.6 = (f32[128,128]{0,1:T(8,128)S(1)}, f32[128,128]{0,1:T(8,128)}, u32[]{:S(2)}) copy-start(f32[128,128]{0,1:T(8,128)} %get-tuple-element.19) | copy-start | bytes 196612
  386.3 29.7 %copy-start.9 = (f32[128,128]{0,1:T(8,128)S(1)}, f32[128,128]{0,1:T(8,128)}, u32[]{:S(2)}) copy-start(f32[128,128]{0,1:T(8,128)} %get-tuple-element.18) | copy-start | bytes 196612
  386.3 29.7 %copy-start.15 = (f32[128,128]{0,1:T(8,128)S(1)}, f32[128,128]{0,1:T(8,128)}, u32[]{:S(2)}) copy-start(f32[128,128]{0,1:T(8,128)} %get-tuple-element.20) | copy-start | bytes 196612
  442.3 39.9 %copy-start.1 = (f32[128,1536]{1,0:T(8,128)S(1)}, f32[128,1536]{1,0:T(8,128)}, u32[]{:S(2)}) copy-start(f32[128,1536]{1,0:T(8,128)} %copy-done) | copy-start | bytes 2359300
  484.1 36.7 %collective-permute-start.2 = (f32[128,1536]{1,0:T(8,128)}, f32[128,1536]{1,0:T(8,128)S(1)}, u32[]{:S(2)}, u32[]{:S(2)}) collective-permute-start(f32[128,1536]{1,0:T(8,128)} %fusion.7), channel_id=1, source_target_pairs={{0,16},{16,0},{4,20},{20,4},{8,24},{24,8},{12,28},{28,12},{1,17},{... | collective-permute-start | bytes 2359304 | tf_op jit(solution)/shard_map/ppermute | solution.py:18
  523.7 158.1 %all-reduce.9.cloned.1.call-start = ((), (), s32[]{:S(2)}) async-start(), calls=%async_computation.1 | async-start | bytes 393216 | tf_op jit(solution)/shard_map/psum | solution.py:94
  567.8 26.7 %copy-start.12 = (f32[128,128]{0,1:T(8,128)S(1)}, f32[128,128]{0,1:T(8,128)}, u32[]{:S(2)}) copy-start(f32[128,128]{0,1:T(8,128)} %get-tuple-element.14) | copy-start | bytes 196612
  567.9 26.7 %copy-start.16 = (f32[128,128]{1,0:T(8,128)S(1)}, f32[128,128]{1,0:T(8,128)}, u32[]{:S(2)}) copy-start(f32[128,128]{1,0:T(8,128)} %get-tuple-element.13) | copy-start | bytes 196612
  595.2 40.1 %copy-start.5 = (f32[128,1536]{1,0:T(8,128)S(1)}, f32[128,1536]{1,0:T(8,128)}, u32[]{:S(2)}) copy-start(f32[128,1536]{1,0:T(8,128)} %copy-done.4) | copy-start | bytes 2359300
  692.1 24.6 %copy-start.18 = (f32[128,256]{1,0:T(8,128)S(1)}, f32[128,256]{1,0:T(8,128)}, u32[]{:S(2)}) copy-start(f32[128,256]{1,0:T(8,128)} %get-tuple-element.10) | copy-start | bytes 393220
  (3 other events, 6.3 us)
Sparse Core Ops, SparseCore 0:
  9.2 29.2 all-gather.2
  112.3 43.3 all-reduce.14
  313.7 44.6 all-reduce.12
  523.8 43.1 all-reduce.10
  639.1 42.6 all-reduce.8
